TPU v7x, 128 devices: a whole 4x4x4 slice. The times are simulated.
128 devices in a mesh: win: 2 (over core), grp: 64 (over z, y, x).
Axes of the slice: x: 4, y: 4, z: 4, core: 2. Of those that a mesh axis runs over, the one named last changes fastest.
Arguments:
- atom_table: float32 [4, 6, 98304], P('win', None, 'grp'), as said below
- row_blocks: int32 [4, 4096], P('win', 'grp'), may hold values from 0 to 767, as said below
- col_blocks: int32 [4, 4096], P('win', 'grp'), may hold values from 0 to 767, as said below
- lambdas: float32 [4], replicated, may hold values from 0 to 1, as said below
- inverse_temp: float32 [1], replicated, may hold values from 20 to 80
- parity: int32 [1], replicated, may hold values from 0 to 1073741823
- thresholds: int32 [4], replicated, may hold values from 0 to 1073741823
Outputs:
- energies: float32 [4, 3], P('win')
- margins: float32 [4], P('win')
- profile: float32 [4], P('win')
Inputs may be any that keep to these rules, and one draw needn't show every extreme that they name: `row_blocks`: the first block of each pair listed on index g of grp lies in that index's share of atoms: blocks g * 12 to (g + 1) * 12 - 1. `col_blocks`: the list of one index of grp names blocks of any one index of grp (itself included) at most 2 times; in each window some index of grp has exactly 2 of its blocks named in every list of that window. `lambdas`: strictly increasing. `atom_table`: field 4 lies in 0.7 to 1.4 and field 5 in 0.6 to 1.4.
All inputs are finite; a program needn't handle non-finite values.
Results may differ from a plain program's by a relative error of at most 0.0003.
Values sent between devices are 32-bit elements; how exact they have to be, the bound alone decides.
A program may use at most 64 MiB of HBM per device.

v0:
```python
import jax
import jax.numpy as jnp
from jax import lax
from jax.sharding import PartitionSpec as P

TILE = 128


tiles_per_step = 16


def from_everyone(shard, axis):
    peers = lax.axis_size(axis)
    return lax.all_to_all(
        jnp.broadcast_to(shard[None], (peers, *shard.shape)), axis, 0, 0, tiled=True
    )


def of_everyone(shard, axis):
    everything = from_everyone(shard, axis)
    return jnp.sum(everything, axis=0)


def from_behind(shard, axis, by):
    peers = lax.axis_size(axis)
    pairs = [(i, i + by) for i in range(peers) if 0 <= i + by < peers]
    return lax.ppermute(shard, axis, pairs)


def combined_pairwise(pieces, combine):
    while len(jax.tree.leaves(pieces)[0]) > 1:
        pieces = jax.vmap(combine)(*(pieces[side::2] for side in (0, 1)))
    return pieces[0]


def carried_in(shard, axis, combine, identity):
    peers, index = (lax.axis_size(axis), lax.axis_index(axis))
    passed = jnp.arange(peers) < index

    def kept(part, zero, own):
        part = jnp.where(
            passed.reshape(-1, *(1 for _ in own.shape)), part, jnp.asarray(zero, own.dtype)
        )
        return part

    pieces = from_everyone(shard, axis)
    return combined_pairwise(kept(pieces, identity, shard), combine)


def pair_energy(row_data, col_data, same_block, lambda_set):
    delta_x = row_data[0][:, :, None] - col_data[0][:, None, :]
    delta_y = row_data[1][:, :, None] - col_data[1][:, None, :]
    delta_z = row_data[2][:, :, None] - col_data[2][:, None, :]
    distance = delta_x * delta_x + delta_y * delta_y + delta_z * delta_z
    charge_pair = row_data[3][:, :, None] * col_data[3][:, None, :]
    well_depth = 4.0 * row_data[4][:, :, None] * col_data[4][:, None, :]
    size_pair = row_data[5][:, :, None] * col_data[5][:, None, :]
    scaled = distance / size_pair
    scaled_cube = scaled * scaled * scaled
    width_tile = distance.shape[-1]
    diagonal = (
        lax.broadcasted_iota(jnp.int32, (width_tile, width_tile), 0)
        == lax.broadcasted_iota(jnp.int32, (width_tile, width_tile), 1)
    ).astype(jnp.float32)
    keep_mask = 1.0 - same_block[:, None, None] * diagonal[None]
    totals = []
    for number in range(3):
        lam_now = lambda_set[number]
        softened = 1.0 - 0.5 * lam_now + scaled_cube
        inverse = 1.0 / softened
        dispersion = well_depth * (inverse * inverse - inverse)
        coulomb = charge_pair * lax.rsqrt(distance + 2.0 - lam_now)
        totals.append(lam_now * jnp.sum(keep_mask * (dispersion + coulomb)))
    return jnp.stack(totals)


def evaluate(row_all, col_all, same_all, lambda_set):
    count = same_all.shape[0] // tiles_per_step

    def advance(number, total):
        start = number * tiles_per_step
        row_part = lax.dynamic_slice_in_dim(row_all, start, tiles_per_step, 1)
        col_part = lax.dynamic_slice_in_dim(col_all, start, tiles_per_step, 1)
        same_part = lax.dynamic_slice_in_dim(same_all, start, tiles_per_step, 0)
        return total + pair_energy(row_part, col_part, same_part, lambda_set)

    return lax.fori_loop(0, count, advance, jnp.zeros((3,), jnp.float32))


def add_terms(earlier, later):
    return earlier + later


def take_blocks(source, indices):
    return jnp.take(source, indices, axis=1)


def per_device(atom_table, row_blocks, col_blocks, lambdas, inverse_temp, parity, thresholds):
    windows = lax.axis_size("win") * atom_table.shape[0]
    groups = lax.axis_size("grp")
    window_run = atom_table.shape[0]
    member = lax.axis_index("grp")
    first_window = lax.axis_index("win") * window_run
    fields = atom_table.shape[1]
    blocks_own = atom_table.reshape(window_run, fields, -1, TILE)
    own_count = blocks_own.shape[2]
    listed = row_blocks.shape[1]
    row_data = jax.vmap(take_blocks)(blocks_own, row_blocks - member * own_count)
    slot_count = max(2, 5 * listed // (4 * groups))
    peers = jnp.arange(groups, dtype=jnp.int32)
    slot_ids = jnp.arange(slot_count, dtype=jnp.int32)

    def plan(col_ids):
        owner_ids = col_ids // own_count
        within_ids = col_ids - owner_ids * own_count
        owner_hot = (owner_ids[:, None] == peers[None, :]).astype(jnp.int32)
        earlier_hot = jnp.cumsum(owner_hot, axis=0) - owner_hot
        order_rank = jnp.sum(earlier_hot * owner_hot, axis=1)
        matched = owner_hot[:, :, None] * (
            order_rank[:, None, None] == slot_ids[None, None, :]
        ).astype(jnp.int32)
        requests = jnp.sum(matched * (within_ids + 1)[:, None, None], axis=0) - 1
        return (owner_ids * slot_count + order_rank, requests)

    positions, requests = jax.vmap(plan)(col_blocks)
    incoming = lax.all_to_all(requests, "grp", split_axis=1, concat_axis=1, tiled=True)

    def answer(source, asked):
        picked = jnp.take(source, jnp.maximum(asked, 0), axis=1)
        return jnp.where((asked >= 0)[None, :, :, None], picked, 0.0)

    replies = jax.vmap(answer)(blocks_own, incoming)
    returned = lax.all_to_all(replies, "grp", split_axis=2, concat_axis=2, tiled=True)
    flat_back = returned.reshape(window_run, fields, groups * slot_count, TILE)
    col_data = jax.vmap(take_blocks)(flat_back, positions)
    same_all = (row_blocks == col_blocks).astype(jnp.float32)
    window = first_window + jnp.arange(window_run, dtype=jnp.int32)
    below = jnp.maximum(window - 1, 0)
    above = jnp.minimum(window + 1, windows - 1)
    lambda_sets = jnp.stack([lambdas[below], lambdas[window], lambdas[above]], axis=1)
    partial_sums = lax.map(
        lambda pack: evaluate(pack[0], pack[1], pack[2], pack[3]),
        (row_data, col_data, same_all, lambda_sets),
    )
    scale_count = listed * groups * TILE * TILE
    lower_win = jnp.where(jnp.remainder(window - parity[0], 2) == 0, window, window - 1)
    upper_win = lower_win + 1
    has_partner = (lower_win >= 0) & (upper_win < windows)
    lower_safe = jnp.clip(lower_win, 0, windows - 1)
    summed = of_everyone(partial_sums, "grp")
    energy = summed / scale_count
    d_plus = energy[:, 2] - energy[:, 1]
    d_minus = energy[:, 0] - energy[:, 1]
    minus_above = from_behind(d_minus[0:1], "win", -1)
    plus_below = from_behind(d_plus[window_run - 1 : window_run], "win", 1)
    minus_next = jnp.concatenate([d_minus[1:], minus_above])
    plus_prev = jnp.concatenate([plus_below, d_plus[:-1]])
    change = jnp.where(lower_win == window, d_plus + minus_next, plus_prev + d_minus)
    carried = carried_in(jnp.sum(d_plus)[None], "win", add_terms, jnp.zeros((1,), jnp.float32))
    profile = carried + (jnp.cumsum(d_plus) - d_plus)
    offset_draw = jnp.remainder(thresholds[lower_safe] + parity[0], 1073741824) + 1
    draw_share = offset_draw.astype(jnp.float32) / 1073741824.0
    margins = jnp.where(has_partner, -jnp.log(draw_share) - inverse_temp[0] * change, 0.0)
    return (energy, margins, profile)


def solution(mesh):
    return jax.shard_map(
        per_device,
        mesh=mesh,
        in_specs=(P("win", None, "grp"), P("win", "grp"), P("win", "grp"), P(), P(), P(), P()),
        out_specs=(P("win", None), P("win"), P("win")),
        check_vma=False,
    )
```

profile of v0, /device:TPU:1, one launch (start us, length us, event | category | flops | bytes accessed | tf_op | source)
XLA Modules:
  0.0 180.5 jit_solution(3026318632566730354)
XLA Ops:
  2.6 12.1 %all-to-all-start = ((s32[2,64,2]{2,0,1:T(2,128)}), s32[2,64,2]{2,0,1:T(2,128)S(1)}, u32[]{:S(2)}, u32[]{:S(2)}) async-start(s32[2,64,2]{2,0,1:T(2,128)} %copy.80), calls=%async_computation | async-start | bytes 131072 | tf_op jit(solution)/shard_map/all_to_all | solution.py:126
  18.2 5.0 %all-to-all-done = s32[2,64,2]{2,0,1:T(2,128)S(1)} async-done(((s32[2,64,2]{2,0,1:T(2,128)}), s32[2,64,2]{2,0,1:T(2,128)S(1)}, u32[]{:S(2)}, u32[]{:S(2)}) %all-to-all-start) | async-done | bytes 1056 | tf_op jit(solution)/shard_map/all_to_all | solution.py:126
  26.7 5.0 %all-to-all-start.1 = ((f32[2,6,64,2,128]{4,3,1,0,2:T(2,128)}), f32[2,6,64,2,128]{4,3,1,0,2:T(2,128)S(1)}, u32[]{:S(2)}, u32[]{:S(2)}) async-start(f32[2,6,64,2,128]{4,3,1,0,2:T(2,128)} %fusion.15), calls=%async_computation.1 | async-start | bytes 1572864 | tf_op jit(solution)/shard_map/all_to_all | solution.py:133
  33.8 11.8 %all-to-all-done.1 = f32[2,6,64,2,128]{4,3,1,0,2:T(2,128)S(1)} async-done(((f32[2,6,64,2,128]{4,3,1,0,2:T(2,128)}), f32[2,6,64,2,128]{4,3,1,0,2:T(2,128)S(1)}, u32[]{:S(2)}, u32[]{:S(2)}) %all-to-all-start.1) | async-done | bytes 786464 | tf_op jit(solution)/shard_map/all_to_all | solution.py:133
  47.0 98.7 %while.27 = (s32[]{:T(128)}, f32[2,3]{1,0:T(2,128)S(1)}, f32[2,6,64,128]{3,2,0,1:T(8,128)S(1)}, f32[2,6,64,128]{3,2,0,1:T(8,128)S(1)}, f32[2,64]{1,0:T(2,128)S(1...) while((s32[]{:T(128)}, f32[2,3]{1,0:T(2,128)S(1)}, ...), condition=%wide.region_9.10_spmd, body=%wide.region_3.0_spmd.sunk | while | flops 16812060 | bytes 1377978 | solution.py:141
  49.7 46.7 %while.28 = (s32[]{:T(128)}, f32[3]{0:T(128)S(1)}, f32[3]{0:T(128)S(1)}, f32[64]{0:T(128)S(1)}, f32[6,64,128]{2,1,0:T(8,128)S(1)}, /*index=5*/f32[6,64,128]{2,1,...) while((s32[]{:T(128)}, f32[3]{0:T(128)S(1)}, ...), condition=%wide.region_8.8_spmd.clone, body=%wide.region_4.7_spmd.clone.sunk | while | flops 16812052 | bytes 590521 | solution.py:87
  50.4 4.0 %fusion.52 = (f32[]{:T(128)}, f32[]{:T(128)}) fusion(f32[]{:T(128)} %bitcast.124, f32[16,128]{1,0:T(8,128)S(1)} %get-tuple-element.515, f32[16,128]{1,0:T(8,128)S(1)} %get-tuple-element.516, f32[16,128]{1,0:T(8,128)S(1)} %get-tuple-element.517, f32[16,128]{1,0:T(8,128)S(1)} %get-tuple-element.518, f32[16,128]{1,0:T(8,128)S(1)} %get-tuple-element.519, ...), kind=kLoop, calls=%fused_computation.19.clone.1 | loop fusion | flops 9699326 | bytes 163928 | tf_op jit(solution)/shard_map/while/body/eval_jaxpr/while/body/eval_jaxpr/reduce_sum | solution.py:73
  55.6 3.3 %fusion.53 = f32[]{:T(128)} fusion(f32[]{:T(128)} %bitcast.126, f32[]{:T(128)} %get-tuple-element.573, f32[16,128]{1,0:T(8,128)S(1)} %get-tuple-element.515, f32[16,128]{1,0:T(8,128)S(1)} %get-tuple-element.516, f32[16,128]{1,0:T(8,128)S(1)} %get-tuple-element.517, f32[16,128]{1,0:T(8,128)S(1)} %get-tuple-element.518, ...), kind=kLoop, calls=%fused_computation.22.clone.1 | loop fusion | flops 7077887 | bytes 163916 | tf_op jit(solution)/shard_map/while/body/eval_jaxpr/while/body/eval_jaxpr/reduce_sum | solution.py:73
  62.1 4.0 %fusion.52 = (f32[]{:T(128)}, f32[]{:T(128)}) fusion(f32[]{:T(128)} %bitcast.124, f32[16,128]{1,0:T(8,128)S(1)} %get-tuple-element.515, f32[16,128]{1,0:T(8,128)S(1)} %get-tuple-element.516, f32[16,128]{1,0:T(8,128)S(1)} %get-tuple-element.517, f32[16,128]{1,0:T(8,128)S(1)} %get-tuple-element.518, f32[16,128]{1,0:T(8,128)S(1)} %get-tuple-element.519, ...), kind=kLoop, calls=%fused_computation.19.clone.1 | loop fusion | flops 9699326 | bytes 163928 | tf_op jit(solution)/shard_map/while/body/eval_jaxpr/while/body/eval_jaxpr/reduce_sum | solution.py:73
  67.3 3.3 %fusion.53 = f32[]{:T(128)} fusion(f32[]{:T(128)} %bitcast.126, f32[]{:T(128)} %get-tuple-element.573, f32[16,128]{1,0:T(8,128)S(1)} %get-tuple-element.515, f32[16,128]{1,0:T(8,128)S(1)} %get-tuple-element.516, f32[16,128]{1,0:T(8,128)S(1)} %get-tuple-element.517, f32[16,128]{1,0:T(8,128)S(1)} %get-tuple-element.518, ...), kind=kLoop, calls=%fused_computation.22.clone.1 | loop fusion | flops 7077887 | bytes 163916 | tf_op jit(solution)/shard_map/while/body/eval_jaxpr/while/body/eval_jaxpr/reduce_sum | solution.py:73
  73.7 4.0 %fusion.52 = (f32[]{:T(128)}, f32[]{:T(128)}) fusion(f32[]{:T(128)} %bitcast.124, f32[16,128]{1,0:T(8,128)S(1)} %get-tuple-element.515, f32[16,128]{1,0:T(8,128)S(1)} %get-tuple-element.516, f32[16,128]{1,0:T(8,128)S(1)} %get-tuple-element.517, f32[16,128]{1,0:T(8,128)S(1)} %get-tuple-element.518, f32[16,128]{1,0:T(8,128)S(1)} %get-tuple-element.519, ...), kind=kLoop, calls=%fused_computation.19.clone.1 | loop fusion | flops 9699326 | bytes 163928 | tf_op jit(solution)/shard_map/while/body/eval_jaxpr/while/body/eval_jaxpr/reduce_sum | solution.py:73
  85.4 4.0 %fusion.52 = (f32[]{:T(128)}, f32[]{:T(128)}) fusion(f32[]{:T(128)} %bitcast.124, f32[16,128]{1,0:T(8,128)S(1)} %get-tuple-element.515, f32[16,128]{1,0:T(8,128)S(1)} %get-tuple-element.516, f32[16,128]{1,0:T(8,128)S(1)} %get-tuple-element.517, f32[16,128]{1,0:T(8,128)S(1)} %get-tuple-element.518, f32[16,128]{1,0:T(8,128)S(1)} %get-tuple-element.519, ...), kind=kLoop, calls=%fused_computation.19.clone.1 | loop fusion | flops 9699326 | bytes 163928 | tf_op jit(solution)/shard_map/while/body/eval_jaxpr/while/body/eval_jaxpr/reduce_sum | solution.py:73
  90.6 3.3 %fusion.53 = f32[]{:T(128)} fusion(f32[]{:T(128)} %bitcast.126, f32[]{:T(128)} %get-tuple-element.573, f32[16,128]{1,0:T(8,128)S(1)} %get-tuple-element.515, f32[16,128]{1,0:T(8,128)S(1)} %get-tuple-element.516, f32[16,128]{1,0:T(8,128)S(1)} %get-tuple-element.517, f32[16,128]{1,0:T(8,128)S(1)} %get-tuple-element.518, ...), kind=kLoop, calls=%fused_computation.22.clone.1 | loop fusion | flops 7077887 | bytes 163916 | tf_op jit(solution)/shard_map/while/body/eval_jaxpr/while/body/eval_jaxpr/reduce_sum | solution.py:73
  99.0 46.7 %while.28 = (s32[]{:T(128)}, f32[3]{0:T(128)S(1)}, f32[3]{0:T(128)S(1)}, f32[64]{0:T(128)S(1)}, f32[6,64,128]{2,1,0:T(8,128)S(1)}, /*index=5*/f32[6,64,128]{2,1,...) while((s32[]{:T(128)}, f32[3]{0:T(128)S(1)}, ...), condition=%wide.region_8.8_spmd.clone, body=%wide.region_4.7_spmd.clone.sunk | while | flops 16812052 | bytes 590521 | solution.py:87
  99.8 4.0 %fusion.52 = (f32[]{:T(128)}, f32[]{:T(128)}) fusion(f32[]{:T(128)} %bitcast.124, f32[16,128]{1,0:T(8,128)S(1)} %get-tuple-element.515, f32[16,128]{1,0:T(8,128)S(1)} %get-tuple-element.516, f32[16,128]{1,0:T(8,128)S(1)} %get-tuple-element.517, f32[16,128]{1,0:T(8,128)S(1)} %get-tuple-element.518, f32[16,128]{1,0:T(8,128)S(1)} %get-tuple-element.519, ...), kind=kLoop, calls=%fused_computation.19.clone.1 | loop fusion | flops 9699326 | bytes 163928 | tf_op jit(solution)/shard_map/while/body/eval_jaxpr/while/body/eval_jaxpr/reduce_sum | solution.py:73
  105.0 3.3 %fusion.53 = f32[]{:T(128)} fusion(f32[]{:T(128)} %bitcast.126, f32[]{:T(128)} %get-tuple-element.573, f32[16,128]{1,0:T(8,128)S(1)} %get-tuple-element.515, f32[16,128]{1,0:T(8,128)S(1)} %get-tuple-element.516, f32[16,128]{1,0:T(8,128)S(1)} %get-tuple-element.517, f32[16,128]{1,0:T(8,128)S(1)} %get-tuple-element.518, ...), kind=kLoop, calls=%fused_computation.22.clone.1 | loop fusion | flops 7077887 | bytes 163916 | tf_op jit(solution)/shard_map/while/body/eval_jaxpr/while/body/eval_jaxpr/reduce_sum | solution.py:73
  111.4 4.0 %fusion.52 = (f32[]{:T(128)}, f32[]{:T(128)}) fusion(f32[]{:T(128)} %bitcast.124, f32[16,128]{1,0:T(8,128)S(1)} %get-tuple-element.515, f32[16,128]{1,0:T(8,128)S(1)} %get-tuple-element.516, f32[16,128]{1,0:T(8,128)S(1)} %get-tuple-element.517, f32[16,128]{1,0:T(8,128)S(1)} %get-tuple-element.518, f32[16,128]{1,0:T(8,128)S(1)} %get-tuple-element.519, ...), kind=kLoop, calls=%fused_computation.19.clone.1 | loop fusion | flops 9699326 | bytes 163928 | tf_op jit(solution)/shard_map/while/body/eval_jaxpr/while/body/eval_jaxpr/reduce_sum | solution.py:73
  116.6 3.3 %fusion.53 = f32[]{:T(128)} fusion(f32[]{:T(128)} %bitcast.126, f32[]{:T(128)} %get-tuple-element.573, f32[16,128]{1,0:T(8,128)S(1)} %get-tuple-element.515, f32[16,128]{1,0:T(8,128)S(1)} %get-tuple-element.516, f32[16,128]{1,0:T(8,128)S(1)} %get-tuple-element.517, f32[16,128]{1,0:T(8,128)S(1)} %get-tuple-element.518, ...), kind=kLoop, calls=%fused_computation.22.clone.1 | loop fusion | flops 7077887 | bytes 163916 | tf_op jit(solution)/shard_map/while/body/eval_jaxpr/while/body/eval_jaxpr/reduce_sum | solution.py:73
  123.1 4.0 %fusion.52 = (f32[]{:T(128)}, f32[]{:T(128)}) fusion(f32[]{:T(128)} %bitcast.124, f32[16,128]{1,0:T(8,128)S(1)} %get-tuple-element.515, f32[16,128]{1,0:T(8,128)S(1)} %get-tuple-element.516, f32[16,128]{1,0:T(8,128)S(1)} %get-tuple-element.517, f32[16,128]{1,0:T(8,128)S(1)} %get-tuple-element.518, f32[16,128]{1,0:T(8,128)S(1)} %get-tuple-element.519, ...), kind=kLoop, calls=%fused_computation.19.clone.1 | loop fusion | flops 9699326 | bytes 163928 | tf_op jit(solution)/shard_map/while/body/eval_jaxpr/while/body/eval_jaxpr/reduce_sum | solution.py:73
  128.3 3.3 %fusion.53 = f32[]{:T(128)} fusion(f32[]{:T(128)} %bitcast.126, f32[]{:T(128)} %get-tuple-element.573, f32[16,128]{1,0:T(8,128)S(1)} %get-tuple-element.515, f32[16,128]{1,0:T(8,128)S(1)} %get-tuple-element.516, f32[16,128]{1,0:T(8,128)S(1)} %get-tuple-element.517, f32[16,128]{1,0:T(8,128)S(1)} %get-tuple-element.518, ...), kind=kLoop, calls=%fused_computation.22.clone.1 | loop fusion | flops 7077887 | bytes 163916 | tf_op jit(solution)/shard_map/while/body/eval_jaxpr/while/body/eval_jaxpr/reduce_sum | solution.py:73
  134.8 4.0 %fusion.52 = (f32[]{:T(128)}, f32[]{:T(128)}) fusion(f32[]{:T(128)} %bitcast.124, f32[16,128]{1,0:T(8,128)S(1)} %get-tuple-element.515, f32[16,128]{1,0:T(8,128)S(1)} %get-tuple-element.516, f32[16,128]{1,0:T(8,128)S(1)} %get-tuple-element.517, f32[16,128]{1,0:T(8,128)S(1)} %get-tuple-element.518, f32[16,128]{1,0:T(8,128)S(1)} %get-tuple-element.519, ...), kind=kLoop, calls=%fused_computation.19.clone.1 | loop fusion | flops 9699326 | bytes 163928 | tf_op jit(solution)/shard_map/while/body/eval_jaxpr/while/body/eval_jaxpr/reduce_sum | solution.py:73
  146.4 4.7 %all-to-all-start.2 = ((f32[64,2,3]{2,1,0:T(2,128)}), f32[64,2,3]{2,1,0:T(2,128)S(1)}, u32[]{:S(2)}, u32[]{:S(2)}) async-start(f32[64,2,3]{2,1,0:T(2,128)} %broadcast_in_dim.96), calls=%async_computation.2 | async-start | bytes 131072 | tf_op jit(solution)/shard_map/all_to_all | solution.py:14
  152.4 7.1 %all-to-all-done.2 = f32[64,2,3]{2,1,0:T(2,128)S(1)} async-done(((f32[64,2,3]{2,1,0:T(2,128)}), f32[64,2,3]{2,1,0:T(2,128)S(1)}, u32[]{:S(2)}, u32[]{:S(2)}) %all-to-all-start.2) | async-done | bytes 1568 | tf_op jit(solution)/shard_map/all_to_all | solution.py:14
  162.3 7.7 %all_to_all.24 = f32[2,1,1]{2,1,0:T(1,128)S(1)} all-to-all(f32[2,1,1]{2,1,0:T(1,128)S(1)} %broadcast_in_dim.98), channel_id=1, replica_groups=mesh['win'=2,'grp'=64] {'win'}, dimensions={0} | all-to-all | bytes 16 | tf_op jit(solution)/shard_map/all_to_all | solution.py:14
  (128 shorter events, 39.4 us)
Async XLA Ops:
  0.6 16.9 %copy-start = (f32[4]{0:T(128)S(1)}, f32[4]{0:T(128)}, u32[]{:S(2)}) copy-start(f32[4]{0:T(128)} %param.14) | copy-start | bytes 52
  2.6 13.5 %copy-start.2 = (f32[2,6,1536]{2,0,1:T(2,128)S(1)}, f32[2,6,1536]{2,0,1:T(2,128)}, u32[]{:S(2)}) copy-start(f32[2,6,1536]{2,0,1:T(2,128)} %param.11) | copy-start | bytes 221188
  2.6 20.5 %all-to-all-start = ((s32[2,64,2]{2,0,1:T(2,128)}), s32[2,64,2]{2,0,1:T(2,128)S(1)}, u32[]{:S(2)}, u32[]{:S(2)}) async-start(s32[2,64,2]{2,0,1:T(2,128)} %copy.80), calls=%async_computation | async-start | bytes 131072 | tf_op jit(solution)/shard_map/all_to_all | solution.py:126
  15.4 0.7 copy-start.4
  26.7 18.9 %all-to-all-start.1 = ((f32[2,6,64,2,128]{4,3,1,0,2:T(2,128)}), f32[2,6,64,2,128]{4,3,1,0,2:T(2,128)S(1)}, u32[]{:S(2)}, u32[]{:S(2)}) async-start(f32[2,6,64,2,128]{4,3,1,0,2:T(2,128)} %fusion.15), calls=%async_computation.1 | async-start | bytes 1572864 | tf_op jit(solution)/shard_map/all_to_all | solution.py:133
  33.1 0.7 copy-start.3
  146.4 13.1 %all-to-all-start.2 = ((f32[64,2,3]{2,1,0:T(2,128)}), f32[64,2,3]{2,1,0:T(2,128)S(1)}, u32[]{:S(2)}, u32[]{:S(2)}) async-start(f32[64,2,3]{2,1,0:T(2,128)} %broadcast_in_dim.96), calls=%async_computation.2 | async-start | bytes 131072 | tf_op jit(solution)/shard_map/all_to_all | solution.py:14
  151.0 0.7 copy-start.1
  171.3 5.4 %collective-permute-start = (f32[1]{0:T(128)}, f32[1]{0:T(128)}, u32[]{:S(2)}, u32[]{:S(2)}) collective-permute-start(f32[1]{0:T(128)} %bitcast.29), channel_id=1, source_target_pairs={{64,0},{65,1},{66,2},{67,3},{68,4},{69,5},{70,6},{71,7},{72,8},{73... | collective-permute-start | bytes 20 | tf_op jit(solution)/shard_map/ppermute | solution.py:27
  174.1 3.2 %collective-permute-start.1 = (f32[1]{0:T(128)}, f32[1]{0:T(128)}, u32[]{:S(2)}, u32[]{:S(2)}) collective-permute-start(f32[1]{0:T(128)} %bitcast.30), channel_id=1, source_target_pairs={{0,64},{1,65},{2,66},{3,67},{4,68},{5,69},{6,70},{7,71},{8,72},{9,... | collective-permute-start | bytes 20 | tf_op jit(solution)/shard_map/ppermute | solution.py:27
where the time goes:
time: 182 us; the launch traced here: 180 us
  other arithmetic  65.9 us (36%)
  loops' own time  32.9 us (18%)
  starting transfers between devices  25.8 us (14%)
  waiting for transfers between devices  24.5 us (13%)
  local copies, waits for them, and re-layouts  20.2 us (11%)
  blocking collectives  7.69 us (4%)
  between operations  3.52 us (2%)
    reduce_sum x16, other arithmetic, pair_energy(): totals.append(lam_now * jnp.sum(keep_mask * (dispersion + coulomb)))  58 us
    another operation x2, loops' own time, evaluate(): return lax.fori_loop(0, count, advance, jnp.zeros((3,), jnp.float32))  28.9 us
    all_to_all x1, starting transfers between devices, per_device(): lax.all_to_all(requests, 'grp', split_axis=1, concat_axis=1, tiled=True)  12.1 us
    all_to_all x1, waiting for transfers between devices, per_device(): lax.all_to_all(replies, 'grp', split_axis=2, concat_axis=2, tiled=True)  11.8 us
    all_to_all x1, blocking collectives, from_everyone(): lax.all_to_all(jnp.broadcast_to(shard[None], (peers, *shard.shape)), axis...  7.69 us
    all_to_all x1, waiting for transfers between devices, from_everyone(): lax.all_to_all(jnp.broadcast_to(shard[None], (peers, *shard.shape)), axis...  7.1 us
    slice x10, local copies, waits for them, and re-layouts, pair_energy(): lam_now = lambda_set[number]  6.13 us
    all_to_all x1, starting transfers between devices, per_device(): lax.all_to_all(replies, 'grp', split_axis=2, concat_axis=2, tiled=True)  4.97 us
  transfers between devices with their start and end apart: 5, of which 4 were waited for; matrix products, arithmetic and copies ran while one was open for 2% of the time, Pallas kernels for 0%

commit v1 on v0

v1 whole, which is shorter than its diff:
```python
import functools

import jax
import jax.numpy as jnp
from jax import lax
from jax.experimental import pallas as pl
from jax.experimental.pallas import tpu as pltpu
from jax.sharding import PartitionSpec as P

TILE = 128
SUB = 8
FIELDS = 6
LINE = 4
SLOTS = 2
MESH = pl.DeviceIdType.MESH


def kernel(
    sizes,
    table_hbm,
    rows_hbm,
    cols_hbm,
    lam_hbm,
    beta_hbm,
    parity_hbm,
    thresh_hbm,
    energy_ref,
    margin_ref,
    profile_ref,
    table,
    rows,
    cols_s,
    cols,
    lam,
    beta,
    parity,
    thresh,
    line_inner,
    line_edge,
    rot,
    req,
    asked,
    pos,
    where_s,
    send_inner,
    send_edge,
    col_inner,
    col_edge,
    part,
    parts,
    local_sem,
    line_send,
    line_recv,
    req_send,
    req_recv,
    rep_send,
    rep_recv,
    sum_send,
    sum_recv,
):
    wins, groups, own, listed = sizes
    lines = groups // LINE
    per_line = LINE * SLOTS
    win = lax.axis_index("win")
    me = lax.axis_index("grp")
    my_line = me // LINE
    my_x = lax.rem(me, LINE)
    inner = 1 - win
    edge = win
    line_buf = (line_inner, line_edge)
    send_buf = (send_inner, send_edge)
    col_buf = (col_inner, col_edge)

    barrier = pltpu.get_barrier_semaphore()

    for step in range(1, lines):
        pl.semaphore_signal(barrier, inc=1, device_id=(win, lax.rem(my_line + step, lines) * LINE + my_x), device_id_type=MESH)
    for step in range(1, LINE):
        pl.semaphore_signal(barrier, inc=1, device_id=(win, my_line * LINE + lax.rem(my_x + step, LINE)), device_id_type=MESH)
    pl.semaphore_signal(barrier, inc=1, device_id=(1 - win, me), device_id_type=MESH)

    local = [
        pltpu.make_async_copy(src, dst, local_sem.at[number])
        for number, (src, dst) in enumerate(
            [
                (cols_hbm, cols),
                (table_hbm, table),
                (rows_hbm, rows),
                (cols_hbm, cols_s),
                (lam_hbm, lam),
                (beta_hbm, beta),
                (parity_hbm, parity),
                (thresh_hbm, thresh),
            ]
        )
    ]
    for copy in local:
        copy.start()

    local[0].wait()
    col_pair = cols[...]
    iota_line = lax.broadcasted_iota(jnp.int32, (lines, listed), 0)
    before = (
        lax.broadcasted_iota(jnp.int32, (listed, listed), 0)
        < lax.broadcasted_iota(jnp.int32, (listed, listed), 1)
    ).astype(jnp.float32)
    slot_iota = lax.broadcasted_iota(jnp.int32, (lines * per_line, listed), 0)
    for order, number in enumerate((inner, edge)):
        ids = jnp.where(number == 0, col_pair[0:1], col_pair[1:2])
        line_ids = jnp.zeros_like(ids)
        for bound in range(1, lines):
            line_ids += (ids >= bound * LINE * own).astype(jnp.int32)
        within = (ids - line_ids * (LINE * own)).astype(jnp.float32)
        hot = (line_ids == iota_line).astype(jnp.float32)
        earlier = jnp.dot(hot, before, preferred_element_type=jnp.float32)
        rank = jnp.sum(hot * earlier, axis=0, keepdims=True).astype(jnp.int32)
        place = line_ids * per_line + rank
        chosen = (place == slot_iota).astype(jnp.float32)
        asks = lax.dot_general(
            within, chosen, (((1,), (1,)), ((), ())), preferred_element_type=jnp.float32
        )
        req[order : order + 1, :] = asks.astype(jnp.int32)
        pos[order : order + 1, :listed] = place
    to_scalar = pltpu.make_async_copy(pos, where_s, local_sem.at[8])
    to_scalar.start()

    local[1].wait()
    for order, number in enumerate((inner, edge)):
        for field in range(FIELDS):
            pair = table[field]
            row = jnp.where(number == 0, pair[0:1], pair[1:2])
            if field == 5:
                row = 1.0 / row
            for block in range(own):
                line_buf[order][my_x * own + block, field : field + 1, :] = row[
                    :, block * TILE : (block + 1) * TILE
                ]

    pl.semaphore_wait(barrier, lines + LINE - 1)

    def plane(step):
        return lax.rem(my_line + step, lines)

    def request(step):
        return pltpu.make_async_remote_copy(
            src_ref=req,
            dst_ref=asked.at[my_line],
            send_sem=req_send,
            recv_sem=req_recv,
            device_id=(win, plane(step) * LINE + my_x),
            device_id_type=MESH,
        )

    for step in range(1, lines):
        request(step).start()
    own_request = pltpu.make_async_copy(req, asked.at[my_line], local_sem.at[9])
    own_request.start()

    def share(order, step):
        return pltpu.make_async_remote_copy(
            src_ref=line_buf[order].at[pl.ds(my_x * own, own)],
            dst_ref=line_buf[order].at[pl.ds(my_x * own, own)],
            send_sem=line_send.at[order],
            recv_sem=line_recv.at[order],
            device_id=(win, my_line * LINE + lax.rem(my_x + step, LINE)),
            device_id_type=MESH,
        )

    for order in range(2):
        for step in (2, 1, 3):
            share(order, step).start()

    def rotate(number, carry):
        for order in range(2):
            block = line_buf[order][my_x * own + number]
            for field in range(FIELDS):
                row = jnp.broadcast_to(block[field : field + 1], (SUB, TILE))
                if field == 4:
                    row = 4.0 * row
                for tile in range(TILE // SUB):
                    rot[order, number, field, tile * SUB : (tile + 1) * SUB, :] = pltpu.roll(
                        row, tile * SUB, 1, stride=1, stride_axis=0
                    )
        return carry

    lax.fori_loop(0, own, rotate, 0)

    for copy in local[2:]:
        copy.wait()
    to_scalar.wait()

    own_request.wait()
    pltpu.make_async_copy(
        asked.at[pl.ds(0, lines - 1)], asked.at[pl.ds(0, lines - 1)], req_recv
    ).wait()

    def reply(order, step):
        return pltpu.make_async_remote_copy(
            src_ref=send_buf[order].at[step - 1],
            dst_ref=col_buf[order].at[pl.ds(my_line * per_line, per_line)],
            send_sem=rep_send.at[order],
            recv_sem=rep_recv.at[order],
            device_id=(win, plane(step) * LINE + my_x),
            device_id_type=MESH,
        )

    for order in range(2):
        pltpu.make_async_copy(
            line_buf[order].at[pl.ds(0, own * (LINE - 1))],
            line_buf[order].at[pl.ds(0, own * (LINE - 1))],
            line_recv.at[order],
        ).wait()

        def serve(step, carry, order=order):
            peer = plane(step)
            for slot in range(per_line):
                wanted = jnp.clip(asked[peer, order, my_line * per_line + slot], 0, LINE * own - 1)
                send_buf[order][step - 1, slot] = line_buf[order][wanted]
            reply(order, step).start()
            return carry

        lax.fori_loop(1, lines, serve, 0)
        for slot in range(per_line):
            wanted = jnp.clip(asked[my_line, order, my_line * per_line + slot], 0, LINE * own - 1)
            col_buf[order][my_line * per_line + slot] = line_buf[order][wanted]

    first_sub = lax.broadcasted_iota(jnp.int32, (SUB, TILE), 0) == 0
    lane = lax.broadcasted_iota(jnp.int32, (1, TILE), 1)
    out_row = jnp.zeros((1, TILE), jnp.float32)
    count = 0
    for order, number in enumerate((inner, edge)):
        pltpu.make_async_copy(
            col_buf[order].at[pl.ds(0, (lines - 1) * per_line)],
            col_buf[order].at[pl.ds(0, (lines - 1) * per_line)],
            rep_recv.at[order],
        ).wait()
        if order == 0:
            lams = [lam[win + k] for k in range(3)]
        else:
            lams = [lam[2 * win + k] for k in range(2)]
        base = [jnp.full((SUB, TILE), 1.0 - 0.5 * l, jnp.float32) for l in lams]
        soft = [jnp.full((SUB, TILE), 2.0 - l, jnp.float32) for l in lams]

        def pair(p, totals, order=order, number=number, base=base, soft=soft):
            row_id = rows[number, p]
            local_row = jnp.clip(row_id - me * own, 0, own - 1)
            same = row_id == cols_s[number, p]
            drop = jnp.where(same, 0.0, 1.0)
            keep = jnp.where(first_sub, drop, 1.0)
            place = jnp.clip(where_s[order, p], 0, lines * per_line - 1)
            tile = col_buf[order][place]
            xj, yj, zj, qj, ej, sj = [
                jnp.broadcast_to(tile[f : f + 1], (SUB, TILE)) for f in range(FIELDS)
            ]
            disp = [jnp.zeros((SUB, TILE), jnp.float32) for _ in base]
            coul = [jnp.zeros((SUB, TILE), jnp.float32) for _ in base]
            for t in range(TILE // SUB):
                span = slice(t * SUB, (t + 1) * SUB)
                dx = rot[order, local_row, 0, span, :] - xj
                dy = rot[order, local_row, 1, span, :] - yj
                dz = rot[order, local_row, 2, span, :] - zj
                qi = rot[order, local_row, 3, span, :]
                ei = rot[order, local_row, 4, span, :]
                si = rot[order, local_row, 5, span, :]
                if t == 0:
                    qi = qi * keep
                    ei = ei * keep
                r2 = dx * dx + dy * dy + dz * dz
                u = r2 * si * sj
                v = u * u * u
                for k in range(len(base)):
                    inv = 1.0 / (base[k] + v)
                    disp[k] += ei * (inv * inv - inv)
                    coul[k] += qi * lax.rsqrt(r2 + soft[k])
            return tuple(
                total + ej * d + qj * c for total, d, c in zip(totals, disp, coul)
            )

        zero = jnp.zeros((SUB, TILE), jnp.float32)
        totals = lax.fori_loop(0, listed, pair, tuple(zero for _ in lams))
        for total, l in zip(totals, lams):
            out_row = jnp.where(lane == count, jnp.sum(total, keepdims=True) * l, out_row)
            count += 1

    flat = win * groups + me
    part[...] = out_row
    parts[flat] = out_row

    def tell(target_win, target):
        return pltpu.make_async_remote_copy(
            src_ref=part,
            dst_ref=parts.at[flat],
            send_sem=sum_send,
            recv_sem=sum_recv,
            device_id=(target_win, target),
            device_id_type=MESH,
        )

    def tell_all(step, carry):
        other = lax.rem(me + step, groups)
        tell(win, other).start()
        tell(1 - win, other).start()
        return carry

    lax.fori_loop(1, groups, tell_all, 0)
    tell(1 - win, me).start()

    pltpu.make_async_copy(asked.at[pl.ds(0, lines - 1)], asked.at[pl.ds(0, lines - 1)], req_send).wait()
    for order in range(2):
        pltpu.make_async_copy(
            line_buf[order].at[pl.ds(0, own * (LINE - 1))],
            line_buf[order].at[pl.ds(0, own * (LINE - 1))],
            line_send.at[order],
        ).wait()
        pltpu.make_async_copy(send_buf[order], send_buf[order], rep_send.at[order]).wait()

    par = parity[0]
    windows = 4
    firsts = [wins * win, wins * win + 1]
    even = lax.rem(par, 2) == 0

    everyone = pltpu.make_async_copy(
        parts.at[pl.ds(0, wins * groups - 1)], parts.at[pl.ds(0, wins * groups - 1)], sum_recv
    )
    lows = []
    logs = []
    for w in firsts:
        same_par = lax.rem(w, 2) == lax.rem(par, 2)
        low = jnp.where(same_par, w, w - 1)
        has = (low >= 0) & (low + 1 < windows)
        safe = jnp.clip(low, 0, windows - 1)
        draw = ((thresh[safe] + par) & 1073741823) + 1
        share_of = jnp.full((SUB, TILE), draw, jnp.int32).astype(jnp.float32) / 1073741824.0
        logs.append(-jnp.log(share_of)[0, 0])
        lows.append((low, has))
    everyone.wait()
    pltpu.make_async_copy(
        parts.at[pl.ds(0, wins * groups - 1)], parts.at[pl.ds(0, wins * groups - 1)], sum_send
    ).wait()

    def total_of(start):
        chains = [parts[start + k] for k in range(8)]
        for n in range(8, groups):
            chains[n % 8] = chains[n % 8] + parts[start + n]
        while len(chains) > 1:
            chains = [chains[2 * n] + chains[2 * n + 1] for n in range(len(chains) // 2)]
        return chains[0] * (1.0 / (listed * groups * TILE * TILE))

    first, second = total_of(0), total_of(groups)
    a = [first[0, k] for k in range(5)]
    b = [second[0, k] for k in range(5)]
    energies = [
        (a[3], a[3], a[4]),
        (a[0], a[1], a[2]),
        (b[0], b[1], b[2]),
        (b[3], b[4], b[4]),
    ]
    up = [e[2] - e[1] for e in energies]
    down = [e[0] - e[1] for e in energies]
    prof = [0.0, up[0], up[0] + up[1], up[0] + up[1] + up[2]]
    changes = [up[n] + down[n + 1] for n in range(3)]
    for n in range(2):
        for k in range(3):
            energy_ref[n, k] = jnp.where(win == 0, energies[n][k], energies[2 + n][k])
        profile_ref[n] = jnp.where(win == 0, prof[n], prof[2 + n])
        low, has = lows[n]
        change = jnp.where(low <= 0, changes[0], jnp.where(low == 1, changes[1], changes[2]))
        margin_ref[n] = jnp.where(has, logs[n] - beta[0] * change, 0.0)


def per_device(atom_table, row_blocks, col_blocks, lambdas, inverse_temp, parity, thresholds):
    wins = lax.axis_size("win")
    groups = lax.axis_size("grp")
    own = atom_table.shape[2] // TILE
    listed = row_blocks.shape[1]
    lines = groups // LINE
    per_line = LINE * SLOTS
    hbm = pl.BlockSpec(memory_space=pl.ANY)
    smem = pl.BlockSpec(memory_space=pltpu.SMEM)
    f32, i32 = jnp.float32, jnp.int32
    return pl.pallas_call(
        functools.partial(kernel, (wins, groups, own, listed)),
        out_shape=(
            jax.ShapeDtypeStruct((2, 3), f32),
            jax.ShapeDtypeStruct((2,), f32),
            jax.ShapeDtypeStruct((2,), f32),
        ),
        in_specs=[hbm] * 7,
        out_specs=(smem, smem, smem),
        scratch_shapes=[
            pltpu.VMEM((FIELDS, 2, own * TILE), f32),
            pltpu.SMEM((2, listed), i32),
            pltpu.SMEM((2, listed), i32),
            pltpu.VMEM((2, listed), i32),
            pltpu.SMEM((4,), f32),
            pltpu.SMEM((1,), f32),
            pltpu.SMEM((1,), i32),
            pltpu.SMEM((4,), i32),
            pltpu.VMEM((LINE * own, FIELDS, TILE), f32),
            pltpu.VMEM((LINE * own, FIELDS, TILE), f32),
            pltpu.VMEM((2, own, FIELDS, TILE, TILE), f32),
            pltpu.VMEM((2, TILE), i32),
            pltpu.SMEM((lines, 2, TILE), i32),
            pltpu.VMEM((2, TILE), i32),
            pltpu.SMEM((2, TILE), i32),
            pltpu.VMEM((lines - 1, per_line, FIELDS, TILE), f32),
            pltpu.VMEM((lines - 1, per_line, FIELDS, TILE), f32),
            pltpu.VMEM((lines * per_line, FIELDS, TILE), f32),
            pltpu.VMEM((lines * per_line, FIELDS, TILE), f32),
            pltpu.VMEM((1, TILE), f32),
            pltpu.VMEM((wins * groups, 1, TILE), f32),
            pltpu.SemaphoreType.DMA((10,)),
            pltpu.SemaphoreType.DMA((2,)),
            pltpu.SemaphoreType.DMA((2,)),
            pltpu.SemaphoreType.DMA,
            pltpu.SemaphoreType.DMA,
            pltpu.SemaphoreType.DMA((2,)),
            pltpu.SemaphoreType.DMA((2,)),
            pltpu.SemaphoreType.DMA,
            pltpu.SemaphoreType.DMA,
        ],
        compiler_params=pltpu.CompilerParams(collective_id=0, has_side_effects=True),
        name="exchange",
    )(
        jnp.transpose(atom_table, (1, 0, 2)),
        row_blocks,
        col_blocks,
        lambdas,
        inverse_temp,
        parity,
        thresholds,
    )


def solution(mesh):
    return jax.shard_map(
        per_device,
        mesh=mesh,
        in_specs=(P("win", None, "grp"), P("win", "grp"), P("win", "grp"), P(), P(), P(), P()),
        out_specs=(P("win", None), P("win"), P("win")),
        check_vma=False,
    )
```

time: 182 us -> 46.7 us (0.26)
  other arithmetic: 65.9 us -> 0 us
  Pallas kernels: 0 us -> 42.2 us
  loops' own time: 32.9 us -> 0 us
  starting transfers between devices: 25.8 us -> 0 us
  waiting for transfers between devices: 24.5 us -> 0 us
  local copies, waits for them, and re-layouts: 20.2 us -> 2.34 us
  blocking collectives: 7.69 us -> 0 us
    reduce_sum x20 -> x0, other arithmetic: 59 us -> none  [the longest x16 58 us: pair_energy(): totals.append(lam_now * jnp.sum(keep_mask * (dispersion + coulomb)))]
    pallas_call x0 -> x1, Pallas kernels: none -> 42.2 us  [per_device(): pl.pallas_call(functools.partial(kernel, (wins, groups, own, listed)), ou...]
    another operation x3 -> x0, loops' own time: 32.9 us -> none  [the longest x2 28.9 us: evaluate(): return lax.fori_loop(0, count, advance, jnp.zeros((3,), jnp.float32))]
    all_to_all x3 -> x0, waiting for transfers between devices: 23.8 us -> none  [the longest x1 11.8 us: per_device(): lax.all_to_all(replies, 'grp', split_axis=2, concat_axis=2, tiled=True)]
    all_to_all x3 -> x0, starting transfers between devices: 21.7 us -> none  [the longest x1 12.1 us: per_device(): lax.all_to_all(requests, 'grp', split_axis=1, concat_axis=1, tiled=True)]
    slice x13 -> x0, local copies, waits for them, and re-layouts: 7.88 us -> none  [the longest x10 6.13 us: pair_energy(): lam_now = lambda_set[number]]
    all_to_all x1 -> x0, blocking collectives: 7.69 us -> none  [from_everyone(): lax.all_to_all(jnp.broadcast_to(shard[None], (peers, *shard.shape)), axis...]
    gather x13 -> x0, local copies, waits for them, and re-layouts: 6.66 us -> none  [the longest x6 2.35 us: take_blocks(): return jnp.take(source, indices, axis=1)]
  transfers between devices with their start and end apart: 5 -> 0, of which waited for: 4 -> 0; matrix products, arithmetic and copies ran while one was open for 2% -> 0% of each run, Pallas kernels for 0% -> 0%
where the time goes in v1:
time: 46.7 us; the launch traced here: 46.5 us
  Pallas kernels  42.2 us (90%)
  local copies, waits for them, and re-layouts  2.34 us (5%)
  between operations  1.94 us (4%)
    pallas_call x1, Pallas kernels, per_device(): pl.pallas_call(functools.partial(kernel, (wins, groups, own, listed)), ou...  42.2 us
    unnamed x9, local copies, waits for them, and re-layouts  2.34 us

profile of v1, /device:TPU:1, one launch (start us, length us, event | category | flops | bytes accessed | tf_op | source)
XLA Modules:
  0.0 46.5 jit_solution(17946810117073553341)
XLA Ops:
  1.9 42.2 %exchange.1 = (f32[2,3]{1,0:T(2,128)}, f32[2]{0:T(128)}, f32[2]{0:T(128)}) custom-call(f32[6,2,1536]{2,1,0:T(2,128)} %bitcast.1, s32[2,64]{1,0:T(2,128)} %rows_hbm.1, s32[2,64]{1,0:T(2,128)} %cols_hbm.1, f32[4]{0:T(128)} %lam_hbm.1, f32[1]{0:T(128)S(6)} %copy.13.beta_hbm, s32[1]{0:T(128)S(6)} %copy.14.parity_hbm, s32[4]{0:T(128)} %thresh_hbm.1), custom_call_target="tpu_custom_call" | custom-call | tf_op jit(solution)/shard_map/exchange/pallas_call | solution.py:381
  44.2 0.0 copy-start
  44.2 0.6 %copy-done = f32[2,3]{1,0:T(2,128)S(1)} copy-done((f32[2,3]{1,0:T(2,128)S(1)}, f32[2,3]{1,0:T(2,128)}, u32[]{:S(2)}) %copy-start) | copy-done | bytes 48
  44.8 0.0 copy-start.2
  44.8 0.6 %copy.15 = f32[2,3]{1,0:T(2,128)} copy(f32[2,3]{1,0:T(2,128)S(1)} %copy-done) | data formatting | bytes 48
  45.4 0.0 copy-done.2
  45.4 0.0 copy-start.1
  45.4 0.5 %copy.16 = f32[2]{0:T(128)} copy(f32[2]{0:T(128)S(1)} %copy-done.2) | data formatting | bytes 16
  45.9 0.1 copy-done.1
  46.0 0.5 %copy.17 = f32[2]{0:T(128)} copy(f32[2]{0:T(128)S(1)} %copy-done.1) | data formatting | bytes 16
Async XLA Ops:
  44.2 0.6 %copy-start = (f32[2,3]{1,0:T(2,128)S(1)}, f32[2,3]{1,0:T(2,128)}, u32[]{:S(2)}) copy-start(f32[2,3]{1,0:T(2,128)} %get-tuple-element.6) | copy-start | bytes 76
  44.8 0.6 %copy-start.2 = (f32[2]{0:T(128)S(1)}, f32[2]{0:T(128)}, u32[]{:S(2)}) copy-start(f32[2]{0:T(128)} %get-tuple-element.7) | copy-start | bytes 28
  45.4 0.6 %copy-start.1 = (f32[2]{0:T(128)S(1)}, f32[2]{0:T(128)}, u32[]{:S(2)}) copy-start(f32[2]{0:T(128)} %get-tuple-element.8) | copy-start | bytes 28

commit v2 on v1

--- a/solution.py
+++ b/solution.py
@@ -13,6 +13,10 @@
 LINE = 4
 SLOTS = 2
 MESH = pl.DeviceIdType.MESH
+
+
+def hops(offset):
+    return min(offset, LINE - offset)
 
 
 def kernel(
@@ -65,18 +69,31 @@
     me = lax.axis_index("grp")
     my_line = me // LINE
     my_x = lax.rem(me, LINE)
+    my_y = lax.rem(my_line, LINE)
+    my_z = my_line // LINE
+    near = sorted(range(1, lines), key=lambda s: hops(s // LINE) + hops(s % LINE))
     inner = 1 - win
     edge = win
     line_buf = (line_inner, line_edge)
     send_buf = (send_inner, send_edge)
     col_buf = (col_inner, col_edge)
 
+    def plane(step):
+        return lax.rem(my_z + step // LINE, LINE) * LINE + lax.rem(my_y + step % LINE, LINE)
+
     barrier = pltpu.get_barrier_semaphore()
 
-    for step in range(1, lines):
-        pl.semaphore_signal(barrier, inc=1, device_id=(win, lax.rem(my_line + step, lines) * LINE + my_x), device_id_type=MESH)
+    for step in reversed(near):
+        pl.semaphore_signal(
+            barrier, inc=1, device_id=(win, plane(step) * LINE + my_x), device_id_type=MESH
+        )
     for step in range(1, LINE):
-        pl.semaphore_signal(barrier, inc=1, device_id=(win, my_line * LINE + lax.rem(my_x + step, LINE)), device_id_type=MESH)
+        pl.semaphore_signal(
+            barrier,
+            inc=1,
+            device_id=(win, my_line * LINE + lax.rem(my_x + step, LINE)),
+            device_id_type=MESH,
+        )
     pl.semaphore_signal(barrier, inc=1, device_id=(1 - win, me), device_id_type=MESH)
 
     local = [
@@ -124,6 +141,23 @@
     to_scalar = pltpu.make_async_copy(pos, where_s, local_sem.at[8])
     to_scalar.start()
 
+    pl.semaphore_wait(barrier, lines + LINE - 1)
+
+    def request(step):
+        return pltpu.make_async_remote_copy(
+            src_ref=req,
+            dst_ref=asked.at[my_line],
+            send_sem=req_send,
+            recv_sem=req_recv.at[my_line],
+            device_id=(win, plane(step) * LINE + my_x),
+            device_id_type=MESH,
+        )
+
+    for step in reversed(near):
+        request(step).start()
+    own_request = pltpu.make_async_copy(req, asked.at[my_line], local_sem.at[9])
+    own_request.start()
+
     local[1].wait()
     for order, number in enumerate((inner, edge)):
         for field in range(FIELDS):
@@ -135,26 +169,6 @@
                 line_buf[order][my_x * own + block, field : field + 1, :] = row[
                     :, block * TILE : (block + 1) * TILE
                 ]
-
-    pl.semaphore_wait(barrier, lines + LINE - 1)
-
-    def plane(step):
-        return lax.rem(my_line + step, lines)
-
-    def request(step):
-        return pltpu.make_async_remote_copy(
-            src_ref=req,
-            dst_ref=asked.at[my_line],
-            send_sem=req_send,
-            recv_sem=req_recv,
-            device_id=(win, plane(step) * LINE + my_x),
-            device_id_type=MESH,
-        )
-
-    for step in range(1, lines):
-        request(step).start()
-    own_request = pltpu.make_async_copy(req, asked.at[my_line], local_sem.at[9])
-    own_request.start()
 
     def share(order, step):
         return pltpu.make_async_remote_copy(
@@ -190,9 +204,6 @@
     to_scalar.wait()
 
     own_request.wait()
-    pltpu.make_async_copy(
-        asked.at[pl.ds(0, lines - 1)], asked.at[pl.ds(0, lines - 1)], req_recv
-    ).wait()
 
     def reply(order, step):
         return pltpu.make_async_remote_copy(
@@ -204,6 +215,8 @@
             device_id_type=MESH,
         )
 
+    for step in near:
+        pltpu.make_async_copy(asked.at[0], asked.at[0], req_recv.at[plane(step)]).wait()
     for order in range(2):
         pltpu.make_async_copy(
             line_buf[order].at[pl.ds(0, own * (LINE - 1))],
@@ -211,15 +224,13 @@
             line_recv.at[order],
         ).wait()
 
-        def serve(step, carry, order=order):
+        for step in reversed(near):
             peer = plane(step)
             for slot in range(per_line):
                 wanted = jnp.clip(asked[peer, order, my_line * per_line + slot], 0, LINE * own - 1)
                 send_buf[order][step - 1, slot] = line_buf[order][wanted]
-            reply(order, step).start()
-            return carry
-
-        lax.fori_loop(1, lines, serve, 0)
+            if order == 0:
+                reply(order, step).start()
         for slot in range(per_line):
             wanted = jnp.clip(asked[my_line, order, my_line * per_line + slot], 0, LINE * own - 1)
             col_buf[order][my_line * per_line + slot] = line_buf[order][wanted]
@@ -235,6 +246,9 @@
             rep_recv.at[order],
         ).wait()
         if order == 0:
+
+            for step in reversed(near):
+                reply(1, step).start()
             lams = [lam[win + k] for k in range(3)]
         else:
             lams = [lam[2 * win + k] for k in range(2)]
@@ -277,7 +291,7 @@
             )
 
         zero = jnp.zeros((SUB, TILE), jnp.float32)
-        totals = lax.fori_loop(0, listed, pair, tuple(zero for _ in lams))
+        totals = lax.fori_loop(0, listed, pair, tuple(zero for _ in lams), unroll=8)
         for total, l in zip(totals, lams):
             out_row = jnp.where(lane == count, jnp.sum(total, keepdims=True) * l, out_row)
             count += 1
@@ -296,14 +310,14 @@
             device_id_type=MESH,
         )
 
-    def tell_all(step, carry):
-        other = lax.rem(me + step, groups)
-        tell(win, other).start()
+    def away(step):
+        return hops(step // (LINE * LINE)) + hops(step // LINE % LINE) + hops(step % LINE)
+
+    for step in sorted(range(groups), key=away, reverse=True):
+        other = plane(step // LINE) * LINE + lax.rem(my_x + step % LINE, LINE)
         tell(1 - win, other).start()
-        return carry
-
-    lax.fori_loop(1, groups, tell_all, 0)
-    tell(1 - win, me).start()
+        if step:
+            tell(win, other).start()
 
     pltpu.make_async_copy(asked.at[pl.ds(0, lines - 1)], asked.at[pl.ds(0, lines - 1)], req_send).wait()
     for order in range(2):
@@ -378,7 +392,7 @@
     hbm = pl.BlockSpec(memory_space=pl.ANY)
     smem = pl.BlockSpec(memory_space=pltpu.SMEM)
     f32, i32 = jnp.float32, jnp.int32
-    return pl.pallas_call(
+    results = pl.pallas_call(
         functools.partial(kernel, (wins, groups, own, listed)),
         out_shape=(
             jax.ShapeDtypeStruct((2, 3), f32),
@@ -413,7 +427,7 @@
             pltpu.SemaphoreType.DMA((2,)),
             pltpu.SemaphoreType.DMA((2,)),
             pltpu.SemaphoreType.DMA,
-            pltpu.SemaphoreType.DMA,
+            pltpu.SemaphoreType.DMA((lines,)),
             pltpu.SemaphoreType.DMA((2,)),
             pltpu.SemaphoreType.DMA((2,)),
             pltpu.SemaphoreType.DMA,
@@ -431,6 +445,22 @@
         thresholds,
     )
 
+    def hand_over(*refs):
+        copies = [pltpu.make_async_copy(refs[n], refs[3 + n], refs[6].at[n]) for n in range(3)]
+        for copy in copies:
+            copy.start()
+        for copy in copies:
+            copy.wait()
+
+    return pl.pallas_call(
+        hand_over,
+        out_shape=tuple(jax.ShapeDtypeStruct(r.shape, r.dtype) for r in results),
+        in_specs=[hbm] * 3,
+        out_specs=(hbm,) * 3,
+        scratch_shapes=[pltpu.SemaphoreType.DMA((3,))],
+        name="hand_over",
+    )(*results)
+
 
 def solution(mesh):
     return jax.shard_map(

time: 46.7 us -> 40.1 us (0.86)
  Pallas kernels: 42.2 us -> 38 us
  local copies, waits for them, and re-layouts: 2.34 us -> 0 us
    pallas_call x1, Pallas kernels: 42.2 us -> 36.8 us  [per_device(): pl.pallas_call(functools.partial(kernel, (wins, groups, own, listed)), ou...]
    unnamed x9 -> x0, local copies, waits for them, and re-layouts: 2.34 us -> none
    pallas_call x0 -> x1, Pallas kernels: none -> 1.19 us  [per_device(): pl.pallas_call(hand_over, out_shape=tuple((jax.ShapeDtypeStruct(r.shape,...]
where the time goes in v2:
time: 40.1 us; the launch traced here: 39.9 us
  Pallas kernels  38 us (95%)
  between operations  1.93 us (5%)
    pallas_call x1, Pallas kernels, per_device(): pl.pallas_call(functools.partial(kernel, (wins, groups, own, listed)), ou...  36.8 us
    pallas_call x1, Pallas kernels, per_device(): pl.pallas_call(hand_over, out_shape=tuple((jax.ShapeDtypeStruct(r.shape,...  1.19 us

profile of v2, /device:TPU:1, one launch (start us, length us, event | category | flops | bytes accessed | tf_op | source)
XLA Modules:
  0.0 39.9 jit_solution(15224921399273371883)
XLA Ops:
  1.9 36.8 %exchange.1 = (f32[2,3]{1,0:T(2,128)}, f32[2]{0:T(128)}, f32[2]{0:T(128)}) custom-call(f32[6,2,1536]{2,1,0:T(2,128)} %bitcast.1, s32[2,64]{1,0:T(2,128)} %rows_hbm.1, s32[2,64]{1,0:T(2,128)} %cols_hbm.1, f32[4]{0:T(128)} %lam_hbm.1, f32[1]{0:T(128)S(6)} %copy.10.beta_hbm, s32[1]{0:T(128)S(6)} %copy.11.parity_hbm, s32[4]{0:T(128)} %thresh_hbm.1), custom_call_target="tpu_custom_call" | custom-call | tf_op jit(solution)/shard_map/exchange/pallas_call | solution.py:395
  38.7 1.2 %hand_over.1 = (f32[2,3]{1,0:T(2,128)}, f32[2]{0:T(128)}, f32[2]{0:T(128)}) custom-call(f32[2,3]{1,0:T(2,128)} %get-tuple-element.6.refs_0_, f32[2]{0:T(128)} %get-tuple-element.7.refs_1_, f32[2]{0:T(128)} %get-tuple-element.8.refs_2_), custom_call_target="tpu_custom_call" | custom-call | tf_op jit(solution)/shard_map/hand_over/pallas_call | solution.py:455

commit v3 on v2

--- a/solution.py
+++ b/solution.py
@@ -83,19 +83,6 @@
 
     barrier = pltpu.get_barrier_semaphore()
 
-    for step in reversed(near):
-        pl.semaphore_signal(
-            barrier, inc=1, device_id=(win, plane(step) * LINE + my_x), device_id_type=MESH
-        )
-    for step in range(1, LINE):
-        pl.semaphore_signal(
-            barrier,
-            inc=1,
-            device_id=(win, my_line * LINE + lax.rem(my_x + step, LINE)),
-            device_id_type=MESH,
-        )
-    pl.semaphore_signal(barrier, inc=1, device_id=(1 - win, me), device_id_type=MESH)
-
     local = [
         pltpu.make_async_copy(src, dst, local_sem.at[number])
         for number, (src, dst) in enumerate(
@@ -113,6 +100,19 @@
     ]
     for copy in local:
         copy.start()
+
+    for step in reversed(near):
+        pl.semaphore_signal(
+            barrier, inc=1, device_id=(win, plane(step) * LINE + my_x), device_id_type=MESH
+        )
+    for step in range(1, LINE):
+        pl.semaphore_signal(
+            barrier,
+            inc=1,
+            device_id=(win, my_line * LINE + lax.rem(my_x + step, LINE)),
+            device_id_type=MESH,
+        )
+    pl.semaphore_signal(barrier, inc=1, device_id=(1 - win, me), device_id_type=MESH)
 
     local[0].wait()
     col_pair = cols[...]
@@ -141,23 +141,6 @@
     to_scalar = pltpu.make_async_copy(pos, where_s, local_sem.at[8])
     to_scalar.start()
 
-    pl.semaphore_wait(barrier, lines + LINE - 1)
-
-    def request(step):
-        return pltpu.make_async_remote_copy(
-            src_ref=req,
-            dst_ref=asked.at[my_line],
-            send_sem=req_send,
-            recv_sem=req_recv.at[my_line],
-            device_id=(win, plane(step) * LINE + my_x),
-            device_id_type=MESH,
-        )
-
-    for step in reversed(near):
-        request(step).start()
-    own_request = pltpu.make_async_copy(req, asked.at[my_line], local_sem.at[9])
-    own_request.start()
-
     local[1].wait()
     for order, number in enumerate((inner, edge)):
         for field in range(FIELDS):
@@ -170,6 +153,23 @@
                     :, block * TILE : (block + 1) * TILE
                 ]
 
+    pl.semaphore_wait(barrier, lines + LINE - 1)
+
+    def request(step):
+        return pltpu.make_async_remote_copy(
+            src_ref=req,
+            dst_ref=asked.at[my_line],
+            send_sem=req_send,
+            recv_sem=req_recv.at[my_line],
+            device_id=(win, plane(step) * LINE + my_x),
+            device_id_type=MESH,
+        )
+
+    for step in reversed(near):
+        request(step).start()
+    own_request = pltpu.make_async_copy(req, asked.at[my_line], local_sem.at[9])
+    own_request.start()
+
     def share(order, step):
         return pltpu.make_async_remote_copy(
             src_ref=line_buf[order].at[pl.ds(my_x * own, own)],
@@ -184,23 +184,40 @@
         for step in (2, 1, 3):
             share(order, step).start()
 
-    def rotate(number, carry):
-        for order in range(2):
-            block = line_buf[order][my_x * own + number]
-            for field in range(FIELDS):
-                row = jnp.broadcast_to(block[field : field + 1], (SUB, TILE))
-                if field == 4:
-                    row = 4.0 * row
-                for tile in range(TILE // SUB):
-                    rot[order, number, field, tile * SUB : (tile + 1) * SUB, :] = pltpu.roll(
-                        row, tile * SUB, 1, stride=1, stride_axis=0
-                    )
-        return carry
-
-    lax.fori_loop(0, own, rotate, 0)
-
     for copy in local[2:]:
         copy.wait()
+
+    lam_sets = [[lam[win + k] for k in range(3)], [lam[2 * win + k] for k in range(2)]]
+
+    def rotate(order):
+        def turn(number, carry):
+            block = line_buf[order][my_x * own + number]
+            root = 2.0 * jnp.sqrt(block[4:5])
+            scale = 1.0 / root
+            turned = [
+                block[0:1],
+                block[1:2],
+                block[2:3],
+                block[3:4],
+                root,
+                block[5:6] * block[5:6] * block[5:6] * scale,
+                scale,
+            ]
+            for field, row in enumerate(turned):
+                row = jnp.broadcast_to(row, (SUB, TILE))
+                for tile in range(TILE // SUB):
+                    span = slice(tile * SUB, (tile + 1) * SUB)
+                    value = pltpu.roll(row, tile * SUB, 1, stride=1, stride_axis=0)
+                    if field < FIELDS:
+                        rot[order, number, field, span, :] = value
+                    else:
+                        for k, l in enumerate(lam_sets[order]):
+                            rot[order, number, field + k, span, :] = value * (1.0 - 0.5 * l)
+            return carry
+
+        lax.fori_loop(0, own, turn, 0)
+
+
     to_scalar.wait()
 
     own_request.wait()
@@ -234,6 +251,9 @@
         for slot in range(per_line):
             wanted = jnp.clip(asked[my_line, order, my_line * per_line + slot], 0, LINE * own - 1)
             col_buf[order][my_line * per_line + slot] = line_buf[order][wanted]
+        if order == 0:
+            rotate(0)
+            rotate(1)
 
     first_sub = lax.broadcasted_iota(jnp.int32, (SUB, TILE), 0) == 0
     lane = lax.broadcasted_iota(jnp.int32, (1, TILE), 1)
@@ -249,13 +269,10 @@
 
             for step in reversed(near):
                 reply(1, step).start()
-            lams = [lam[win + k] for k in range(3)]
-        else:
-            lams = [lam[2 * win + k] for k in range(2)]
-        base = [jnp.full((SUB, TILE), 1.0 - 0.5 * l, jnp.float32) for l in lams]
+        lams = lam_sets[order]
         soft = [jnp.full((SUB, TILE), 2.0 - l, jnp.float32) for l in lams]
 
-        def pair(p, totals, order=order, number=number, base=base, soft=soft):
+        def pair(p, totals, order=order, number=number, soft=soft):
             row_id = rows[number, p]
             local_row = jnp.clip(row_id - me * own, 0, own - 1)
             same = row_id == cols_s[number, p]
@@ -266,25 +283,25 @@
             xj, yj, zj, qj, ej, sj = [
                 jnp.broadcast_to(tile[f : f + 1], (SUB, TILE)) for f in range(FIELDS)
             ]
-            disp = [jnp.zeros((SUB, TILE), jnp.float32) for _ in base]
-            coul = [jnp.zeros((SUB, TILE), jnp.float32) for _ in base]
+            disp = [jnp.zeros((SUB, TILE), jnp.float32) for _ in soft]
+            coul = [jnp.zeros((SUB, TILE), jnp.float32) for _ in soft]
             for t in range(TILE // SUB):
                 span = slice(t * SUB, (t + 1) * SUB)
                 dx = rot[order, local_row, 0, span, :] - xj
                 dy = rot[order, local_row, 1, span, :] - yj
                 dz = rot[order, local_row, 2, span, :] - zj
                 qi = rot[order, local_row, 3, span, :]
-                ei = rot[order, local_row, 4, span, :]
-                si = rot[order, local_row, 5, span, :]
+                gi = rot[order, local_row, 4, span, :]
+                ai = rot[order, local_row, 5, span, :]
+                r2 = dx * dx + dy * dy + dz * dz
+                u = r2 * sj
+                v = u * u * u * ai
                 if t == 0:
                     qi = qi * keep
-                    ei = ei * keep
-                r2 = dx * dx + dy * dy + dz * dz
-                u = r2 * si * sj
-                v = u * u * u
-                for k in range(len(base)):
-                    inv = 1.0 / (base[k] + v)
-                    disp[k] += ei * (inv * inv - inv)
+                for k in range(len(soft)):
+                    w = 1.0 / (rot[order, local_row, FIELDS + k, span, :] + v)
+                    g = w * (w - gi)
+                    disp[k] += g * keep if t == 0 else g
                     coul[k] += qi * lax.rsqrt(r2 + soft[k])
             return tuple(
                 total + ej * d + qj * c for total, d, c in zip(totals, disp, coul)
@@ -412,7 +429,7 @@
             pltpu.SMEM((4,), i32),
             pltpu.VMEM((LINE * own, FIELDS, TILE), f32),
             pltpu.VMEM((LINE * own, FIELDS, TILE), f32),
-            pltpu.VMEM((2, own, FIELDS, TILE, TILE), f32),
+            pltpu.VMEM((2, own, FIELDS + 3, TILE, TILE), f32),
             pltpu.VMEM((2, TILE), i32),
             pltpu.SMEM((lines, 2, TILE), i32),
             pltpu.VMEM((2, TILE), i32),

time: 40.1 us -> 39.1 us (0.975)
  Pallas kernels: 38 us -> 37.1 us
    pallas_call x1, Pallas kernels: 36.8 us -> 35.9 us  [per_device(): pl.pallas_call(functools.partial(kernel, (wins, groups, own, listed)), ou...]
where the time goes in v3:
time: 39.1 us; the launch traced here: 39 us
  Pallas kernels  37.1 us (95%)
  between operations  1.93 us (5%)
    pallas_call x1, Pallas kernels, per_device(): pl.pallas_call(functools.partial(kernel, (wins, groups, own, listed)), ou...  35.9 us
    pallas_call x1, Pallas kernels, per_device(): pl.pallas_call(hand_over, out_shape=tuple((jax.ShapeDtypeStruct(r.shape,...  1.19 us

profile of v3, /device:TPU:1, one launch (start us, length us, event | category | flops | bytes accessed | tf_op | source)
XLA Modules:
  0.0 39.0 jit_solution(1648248446915637544)
XLA Ops:
  1.9 35.9 %exchange.1 = (f32[2,3]{1,0:T(2,128)}, f32[2]{0:T(128)}, f32[2]{0:T(128)}) custom-call(f32[6,2,1536]{2,1,0:T(2,128)} %bitcast.1, s32[2,64]{1,0:T(2,128)} %rows_hbm.1, s32[2,64]{1,0:T(2,128)} %cols_hbm.1, f32[4]{0:T(128)} %lam_hbm.1, f32[1]{0:T(128)S(6)} %copy.10.beta_hbm, s32[1]{0:T(128)S(6)} %copy.11.parity_hbm, s32[4]{0:T(128)} %thresh_hbm.1), custom_call_target="tpu_custom_call" | custom-call | tf_op jit(solution)/shard_map/exchange/pallas_call | solution.py:412
  37.8 1.2 %hand_over.1 = (f32[2,3]{1,0:T(2,128)}, f32[2]{0:T(128)}, f32[2]{0:T(128)}) custom-call(f32[2,3]{1,0:T(2,128)} %get-tuple-element.6.refs_0_, f32[2]{0:T(128)} %get-tuple-element.7.refs_1_, f32[2]{0:T(128)} %get-tuple-element.8.refs_2_), custom_call_target="tpu_custom_call" | custom-call | tf_op jit(solution)/shard_map/hand_over/pallas_call | solution.py:472

commit v4 on v3

--- a/solution.py
+++ b/solution.py
@@ -121,7 +121,8 @@
         lax.broadcasted_iota(jnp.int32, (listed, listed), 0)
         < lax.broadcasted_iota(jnp.int32, (listed, listed), 1)
     ).astype(jnp.float32)
-    slot_iota = lax.broadcasted_iota(jnp.int32, (lines * per_line, listed), 0)
+    slot_iota = lax.broadcasted_iota(jnp.int32, (TILE, listed), 0)
+    asks = jnp.zeros((lines, TILE), jnp.float32)
     for order, number in enumerate((inner, edge)):
         ids = jnp.where(number == 0, col_pair[0:1], col_pair[1:2])
         line_ids = jnp.zeros_like(ids)
@@ -132,12 +133,14 @@
         earlier = jnp.dot(hot, before, preferred_element_type=jnp.float32)
         rank = jnp.sum(hot * earlier, axis=0, keepdims=True).astype(jnp.int32)
         place = line_ids * per_line + rank
-        chosen = (place == slot_iota).astype(jnp.float32)
-        asks = lax.dot_general(
-            within, chosen, (((1,), (1,)), ((), ())), preferred_element_type=jnp.float32
-        )
-        req[order : order + 1, :] = asks.astype(jnp.int32)
+        ranked = (rank + order * per_line == slot_iota).astype(jnp.float32)
+        asks += lax.dot_general(
+            hot * within, ranked, (((1,), (1,)), ((), ())), preferred_element_type=jnp.float32
+        )
         pos[order : order + 1, :listed] = place
+    asks = asks.astype(jnp.int32)
+    for line in range(lines):
+        req[line] = asks[line : line + 1]
     to_scalar = pltpu.make_async_copy(pos, where_s, local_sem.at[8])
     to_scalar.start()
 
@@ -157,7 +160,7 @@
 
     def request(step):
         return pltpu.make_async_remote_copy(
-            src_ref=req,
+            src_ref=req.at[plane(step)],
             dst_ref=asked.at[my_line],
             send_sem=req_send,
             recv_sem=req_recv.at[my_line],
@@ -167,7 +170,7 @@
 
     for step in reversed(near):
         request(step).start()
-    own_request = pltpu.make_async_copy(req, asked.at[my_line], local_sem.at[9])
+    own_request = pltpu.make_async_copy(req.at[my_line], asked.at[my_line], local_sem.at[9])
     own_request.start()
 
     def share(order, step):
@@ -244,12 +247,12 @@
         for step in reversed(near):
             peer = plane(step)
             for slot in range(per_line):
-                wanted = jnp.clip(asked[peer, order, my_line * per_line + slot], 0, LINE * own - 1)
+                wanted = jnp.clip(asked[peer, 0, order * per_line + slot], 0, LINE * own - 1)
                 send_buf[order][step - 1, slot] = line_buf[order][wanted]
             if order == 0:
                 reply(order, step).start()
         for slot in range(per_line):
-            wanted = jnp.clip(asked[my_line, order, my_line * per_line + slot], 0, LINE * own - 1)
+            wanted = jnp.clip(asked[my_line, 0, order * per_line + slot], 0, LINE * own - 1)
             col_buf[order][my_line * per_line + slot] = line_buf[order][wanted]
         if order == 0:
             rotate(0)
@@ -365,9 +368,6 @@
         logs.append(-jnp.log(share_of)[0, 0])
         lows.append((low, has))
     everyone.wait()
-    pltpu.make_async_copy(
-        parts.at[pl.ds(0, wins * groups - 1)], parts.at[pl.ds(0, wins * groups - 1)], sum_send
-    ).wait()
 
     def total_of(start):
         chains = [parts[start + k] for k in range(8)]
@@ -397,6 +397,9 @@
         low, has = lows[n]
         change = jnp.where(low <= 0, changes[0], jnp.where(low == 1, changes[1], changes[2]))
         margin_ref[n] = jnp.where(has, logs[n] - beta[0] * change, 0.0)
+    pltpu.make_async_copy(
+        parts.at[pl.ds(0, wins * groups - 1)], parts.at[pl.ds(0, wins * groups - 1)], sum_send
+    ).wait()
 
 
 def per_device(atom_table, row_blocks, col_blocks, lambdas, inverse_temp, parity, thresholds):
@@ -430,8 +433,8 @@
             pltpu.VMEM((LINE * own, FIELDS, TILE), f32),
             pltpu.VMEM((LINE * own, FIELDS, TILE), f32),
             pltpu.VMEM((2, own, FIELDS + 3, TILE, TILE), f32),
-            pltpu.VMEM((2, TILE), i32),
-            pltpu.SMEM((lines, 2, TILE), i32),
+            pltpu.VMEM((lines, 1, TILE), i32),
+            pltpu.SMEM((lines, 1, TILE), i32),
             pltpu.VMEM((2, TILE), i32),
             pltpu.SMEM((2, TILE), i32),
             pltpu.VMEM((lines - 1, per_line, FIELDS, TILE), f32),

time: 39.1 us -> 39.1 us (level)
  no operation moved by 1% of the time
where the time goes in v4:
time: 39.1 us; the launch traced here: 38.9 us
  Pallas kernels  37 us (95%)
  between operations  1.93 us (5%)
    pallas_call x1, Pallas kernels, per_device(): pl.pallas_call(functools.partial(kernel, (wins, groups, own, listed)), ou...  35.8 us
    pallas_call x1, Pallas kernels, per_device(): pl.pallas_call(hand_over, out_shape=tuple((jax.ShapeDtypeStruct(r.shape,...  1.19 us

profile of v4, /device:TPU:1, one launch (start us, length us, event | category | flops | bytes accessed | tf_op | source)
XLA Modules:
  0.0 38.9 jit_solution(2519716311105303620)
XLA Ops:
  1.9 35.8 %exchange.1 = (f32[2,3]{1,0:T(2,128)}, f32[2]{0:T(128)}, f32[2]{0:T(128)}) custom-call(f32[6,2,1536]{2,1,0:T(2,128)} %bitcast.1, s32[2,64]{1,0:T(2,128)} %rows_hbm.1, s32[2,64]{1,0:T(2,128)} %cols_hbm.1, f32[4]{0:T(128)} %lam_hbm.1, f32[1]{0:T(128)S(6)} %copy.10.beta_hbm, s32[1]{0:T(128)S(6)} %copy.11.parity_hbm, s32[4]{0:T(128)} %thresh_hbm.1), custom_call_target="tpu_custom_call" | custom-call | tf_op jit(solution)/shard_map/exchange/pallas_call | solution.py:415
  37.7 1.2 %hand_over.1 = (f32[2,3]{1,0:T(2,128)}, f32[2]{0:T(128)}, f32[2]{0:T(128)}) custom-call(f32[2,3]{1,0:T(2,128)} %get-tuple-element.6.refs_0_, f32[2]{0:T(128)} %get-tuple-element.7.refs_1_, f32[2]{0:T(128)} %get-tuple-element.8.refs_2_), custom_call_target="tpu_custom_call" | custom-call | tf_op jit(solution)/shard_map/hand_over/pallas_call | solution.py:475

commit v5 on v4

--- a/solution.py
+++ b/solution.py
@@ -183,9 +183,8 @@
             device_id_type=MESH,
         )
 
-    for order in range(2):
-        for step in (2, 1, 3):
-            share(order, step).start()
+    for step in (2, 1, 3):
+        share(0, step).start()
 
     for copy in local[2:]:
         copy.wait()
@@ -251,6 +250,9 @@
                 send_buf[order][step - 1, slot] = line_buf[order][wanted]
             if order == 0:
                 reply(order, step).start()
+        if order == 0:
+            for step in (2, 1, 3):
+                share(1, step).start()
         for slot in range(per_line):
             wanted = jnp.clip(asked[my_line, 0, order * per_line + slot], 0, LINE * own - 1)
             col_buf[order][my_line * per_line + slot] = line_buf[order][wanted]
@@ -313,7 +315,7 @@
         zero = jnp.zeros((SUB, TILE), jnp.float32)
         totals = lax.fori_loop(0, listed, pair, tuple(zero for _ in lams), unroll=8)
         for total, l in zip(totals, lams):
-            out_row = jnp.where(lane == count, jnp.sum(total, keepdims=True) * l, out_row)
+            out_row = jnp.where(lane == count, jnp.sum(jnp.sum(total, axis=0, keepdims=True), axis=1, keepdims=True) * l, out_row)
             count += 1
 
     flat = win * groups + me

time: 39.1 us -> 39 us (level)
  no operation moved by 1% of the time
where the time goes in v5:
time: 39 us; the launch traced here: 38.9 us
  Pallas kernels  36.9 us (95%)
  between operations  1.93 us (5%)
    pallas_call x1, Pallas kernels, per_device(): pl.pallas_call(functools.partial(kernel, (wins, groups, own, listed)), ou...  35.7 us
    pallas_call x1, Pallas kernels, per_device(): pl.pallas_call(hand_over, out_shape=tuple((jax.ShapeDtypeStruct(r.shape,...  1.19 us

profile of v5, /device:TPU:1, one launch (start us, length us, event | category | flops | bytes accessed | tf_op | source)
XLA Modules:
  0.0 38.9 jit_solution(17604528690620732229)
XLA Ops:
  1.9 35.7 %exchange.1 = (f32[2,3]{1,0:T(2,128)}, f32[2]{0:T(128)}, f32[2]{0:T(128)}) custom-call(f32[6,2,1536]{2,1,0:T(2,128)} %bitcast.1, s32[2,64]{1,0:T(2,128)} %rows_hbm.1, s32[2,64]{1,0:T(2,128)} %cols_hbm.1, f32[4]{0:T(128)} %lam_hbm.1, f32[1]{0:T(128)S(6)} %copy.10.beta_hbm, s32[1]{0:T(128)S(6)} %copy.11.parity_hbm, s32[4]{0:T(128)} %thresh_hbm.1), custom_call_target="tpu_custom_call" | custom-call | tf_op jit(solution)/shard_map/exchange/pallas_call | solution.py:417
  37.7 1.2 %hand_over.1 = (f32[2,3]{1,0:T(2,128)}, f32[2]{0:T(128)}, f32[2]{0:T(128)}) custom-call(f32[2,3]{1,0:T(2,128)} %get-tuple-element.6.refs_0_, f32[2]{0:T(128)} %get-tuple-element.7.refs_1_, f32[2]{0:T(128)} %get-tuple-element.8.refs_2_), custom_call_target="tpu_custom_call" | custom-call | tf_op jit(solution)/shard_map/hand_over/pallas_call | solution.py:477
